TPU v7x, 32 devices: a whole 2x2x4 slice. The times are simulated.
32 devices in a mesh: fsdp: 2 (over core), ctx: 4 (over y, x), tensor: 4 (over z).
Axes of the slice: x: 2, y: 2, z: 4, core: 2. Of those that a mesh axis runs over, the one named last changes fastest.
Arguments:
- tokens: bfloat16 [4, 1024, 2048], P('fsdp', ('ctx', 'tensor')), may hold values from -6 to 6
- segments: int32 [4, 1024], P('fsdp'), may hold values from 0 to 6, as said below
- positions: int32 [4, 1024], P('fsdp'), may hold values from 0 to 1226, as said below
- query_weight: bfloat16 [2048, 2048], P(('fsdp', 'ctx'), 'tensor'), may hold values from -0.125 to 0.125
- key_weight: bfloat16 [2048, 2048], P(('fsdp', 'ctx'), 'tensor'), may hold values from -0.125 to 0.125
- value_weight: bfloat16 [2048, 2048], P(('fsdp', 'ctx'), 'tensor'), may hold values from -0.125 to 0.125
- output_weight: bfloat16 [2048, 2048], P(('fsdp', 'ctx'), 'tensor'), may hold values from -0.125 to 0.125
- gate_weight: bfloat16 [2048, 8192], P(('fsdp', 'ctx'), 'tensor'), may hold values from -0.125 to 0.125
- up_projection_weight: bfloat16 [2048, 8192], P(('fsdp', 'ctx'), 'tensor'), may hold values from -0.125 to 0.125
- down_weight: bfloat16 [2048, 8192], P(('fsdp', 'ctx'), 'tensor'), may hold values from -0.0625 to 0.0625
- query_gain: float32 [2048], replicated, may hold values from 0.5 to 1.5
- key_gain: float32 [2048], replicated, may hold values from 0.5 to 1.5
- attention_gain: float32 [2048], replicated, may hold values from 0.5 to 1.5
- feedforward_gain: float32 [2048], replicated, may hold values from 0.5 to 1.5
- cotangent: bfloat16 [4, 1024, 2048], P('fsdp', ('ctx', 'tensor')), may hold values from -6 to 6
Outputs:
- block_out: bfloat16 [4, 1024, 2048], P('fsdp', ('ctx', 'tensor'))
- input_grad: float32 [4, 1024, 2048], P('fsdp', ('ctx', 'tensor'))
- query_weight_grad: float32 [2048, 2048], P(('fsdp', 'ctx'), 'tensor')
- key_weight_grad: float32 [2048, 2048], P(('fsdp', 'ctx'), 'tensor')
- value_weight_grad: float32 [2048, 2048], P(('fsdp', 'ctx'), 'tensor')
- output_weight_grad: float32 [2048, 2048], P(('fsdp', 'ctx'), 'tensor')
- gate_weight_grad: float32 [2048, 8192], P(('fsdp', 'ctx'), 'tensor')
- up_weight_grad: float32 [2048, 8192], P(('fsdp', 'ctx'), 'tensor')
- down_weight_grad: float32 [2048, 8192], P(('fsdp', 'ctx'), 'tensor')
- query_gain_grad: float32 [2048], replicated
- key_gain_grad: float32 [2048], replicated
- attention_gain_grad: float32 [2048], replicated
- feedforward_gain_grad: float32 [2048], replicated
Inputs may be any that keep to these rules, and one draw needn't show every extreme that they name: `segments`: in each sequence the numbers start at 0 and rise by one where a new document begins; documents hold a fifth of 1024 (rounded down) to 2047 tokens, and the first may have begun before the sequence. `positions`: each token's index in its document; it rises by one from token to token within a document and is 0 where a document begins inside the sequence.
All inputs are finite; a program needn't handle non-finite values.
Results may differ from a plain program's by a relative error of at most 0.017.
Values may be sent and summed in bfloat16 or wider, within the bound.
A program may use at most 256 MiB of HBM per device.

v0:
```python
import jax
import jax.numpy as jnp
from jax import lax
from jax.sharding import PartitionSpec as P

D = 2048
HD = 128
epsilon = 1e-06
rope_theta = 500000.0
masked_score = -1e30


def rope_tables(position_ids):
    freq_index = jnp.arange(HD // 2, dtype=jnp.float32)
    inverse = rope_theta ** (-2.0 * freq_index / HD)
    angles = position_ids.astype(jnp.float32)[..., None] * inverse
    return (jnp.cos(angles), jnp.sin(angles))


def rotate(values, cosine, sine):
    half = values.shape[-1] // 2
    first_half = values[..., :half]
    second_half = values[..., half:]
    cos_wide = cosine[..., None, :]
    sin_wide = sine[..., None, :]
    return jnp.concatenate(
        [
            first_half * cos_wide - second_half * sin_wide,
            second_half * cos_wide + first_half * sin_wide,
        ],
        axis=-1,
    )


def unrotate(values, cosine, sine):
    half = values.shape[-1] // 2
    first_half = values[..., :half]
    second_half = values[..., half:]
    cos_wide = cosine[..., None, :]
    sin_wide = sine[..., None, :]
    return jnp.concatenate(
        [
            first_half * cos_wide + second_half * sin_wide,
            second_half * cos_wide - first_half * sin_wide,
        ],
        axis=-1,
    )


def root_mean_square_scale(values):
    return lax.rsqrt(jnp.mean(values * values, axis=-1, keepdims=True) + epsilon)


def norm_back(grad_unit, unit, scale):
    return scale * (grad_unit - unit * jnp.mean(grad_unit * unit, axis=-1, keepdims=True))


def project(matrix_rows, weight_matrix):
    return jnp.einsum("xmj,je->xme", matrix_rows, weight_matrix, preferred_element_type=jnp.float32)


def project_back(matrix_rows, weight_matrix):
    return jnp.einsum("rhy,iy->rhi", matrix_rows, weight_matrix, preferred_element_type=jnp.float32)


def weight_term(left_operand_rows, right_operand_rows):
    return jnp.einsum(
        "prt,pre->te", left_operand_rows, right_operand_rows, preferred_element_type=jnp.float32
    )


def gather_tokens(matrix_rows):
    return lax.all_gather(matrix_rows, "tensor", axis=1, tiled=True)


def sum_tokens(terms):
    return lax.psum_scatter(terms, "tensor", scatter_dimension=1, tiled=True)


def body(
    tokens,
    segments,
    positions,
    query_weight,
    key_weight,
    value_weight,
    output_weight,
    gate_weight,
    up_projection_weight,
    down_weight,
    query_gain,
    key_gain,
    attention_gain,
    feedforward_gain,
    cotangent,
):
    ctx_index = lax.axis_index("ctx")
    tensor_index = lax.axis_index("tensor")
    gathered = (
        lax.all_gather(query_weight, ("fsdp", "ctx"), axis=0, tiled=True),
        lax.all_gather(key_weight, ("fsdp", "ctx"), axis=0, tiled=True),
        lax.all_gather(value_weight, ("fsdp", "ctx"), axis=0, tiled=True),
        lax.all_gather(output_weight, ("fsdp", "ctx"), axis=0, tiled=True),
        lax.all_gather(gate_weight, ("fsdp", "ctx"), axis=0, tiled=True),
        lax.all_gather(up_projection_weight, ("fsdp", "ctx"), axis=0, tiled=True),
        lax.all_gather(down_weight, ("fsdp", "ctx"), axis=0, tiled=True),
    )
    query_full, key_full, value_full, output_full, gate_full, up_full, down_full = gathered
    width_local = query_full.shape[1]
    heads_local = width_local // HD
    gain_start = tensor_index * width_local
    query_gain_local = lax.dynamic_slice_in_dim(query_gain, gain_start, width_local)
    key_gain_local = lax.dynamic_slice_in_dim(key_gain, gain_start, width_local)
    score_scale = HD ** (-0.5)
    tokens_block = gather_tokens(tokens)
    seq_count = tokens_block.shape[0]
    block_len = tokens_block.shape[1]
    full_len = segments.shape[1]
    query_lin = project(tokens_block, query_full)
    key_lin = project(tokens_block, key_full)
    value_lin = project(tokens_block, value_full)
    query_squared, key_sq = lax.psum(
        (jnp.sum(query_lin * query_lin, axis=-1), jnp.sum(key_lin * key_lin, axis=-1)), "tensor"
    )
    query_scale = lax.rsqrt(query_squared / D + epsilon)[..., None]
    key_scale = lax.rsqrt(key_sq / D + epsilon)[..., None]
    query_unit = query_lin * query_scale
    key_unit = key_lin * key_scale
    block_pos = lax.dynamic_slice_in_dim(positions, ctx_index * block_len, block_len, 1)
    cosine, sine = rope_tables(block_pos)

    def heads_of(values):
        return values.reshape(seq_count, block_len, heads_local, HD)

    query_rot = rotate(heads_of(query_unit * query_gain_local), cosine, sine).astype(jnp.bfloat16)
    key_rot = rotate(heads_of(key_unit * key_gain_local), cosine, sine).astype(jnp.bfloat16)
    value_rot = heads_of(value_lin).astype(jnp.bfloat16)
    query_heads, key_heads, value_heads = (
        lax.all_to_all(query_rot, "ctx", split_axis=2, concat_axis=1, tiled=True),
        lax.all_to_all(key_rot, "ctx", split_axis=2, concat_axis=1, tiled=True),
        lax.all_to_all(value_rot, "ctx", split_axis=2, concat_axis=1, tiled=True),
    )
    token_index = jnp.arange(full_len, dtype=jnp.int32)
    allowed = (segments[:, :, None] == segments[:, None, :]) & (
        token_index[None, :, None] >= token_index[None, None, :]
    )
    allowed = allowed[:, None]

    def masked_scores():
        raw_scores = (
            jnp.einsum(
                "sqhd,skhd->shqk", query_heads, key_heads, preferred_element_type=jnp.float32
            )
            * score_scale
        )
        return jnp.where(allowed, raw_scores, masked_score)

    scores = masked_scores()
    top_score = jnp.max(scores, axis=-1, keepdims=True)
    log_total = top_score + jnp.log(jnp.sum(jnp.exp(scores - top_score), axis=-1, keepdims=True))
    probs_b = jnp.exp(scores - log_total).astype(jnp.bfloat16)
    attended = jnp.einsum(
        "shqk,skhd->sqhd", probs_b, value_heads, preferred_element_type=jnp.float32
    ).astype(jnp.bfloat16)
    attended_block = lax.all_to_all(
        attended, "ctx", split_axis=1, concat_axis=2, tiled=True
    ).reshape(seq_count, block_len, width_local)
    attention_out = sum_tokens(project_back(attended_block, output_full))
    attention_scale = root_mean_square_scale(attention_out)
    attention_unit = attention_out * attention_scale
    hidden_state = tokens.astype(jnp.float32) + attention_unit * attention_gain
    hidden_block = gather_tokens(hidden_state.astype(jnp.bfloat16))
    gate_lin = project(hidden_block, gate_full)
    up_lin = project(hidden_block, up_full)
    gate_sig = jax.nn.sigmoid(gate_lin)
    gate_act = gate_lin * gate_sig
    mixed = (gate_act * up_lin).astype(jnp.bfloat16)
    mixed_out = sum_tokens(project_back(mixed, down_full))
    mixed_scale = root_mean_square_scale(mixed_out)
    mixed_unit = mixed_out * mixed_scale
    block_out = (hidden_state + mixed_unit * feedforward_gain).astype(jnp.bfloat16)
    back_weights = (
        lax.all_gather(query_weight, ("fsdp", "ctx"), axis=0, tiled=True),
        lax.all_gather(key_weight, ("fsdp", "ctx"), axis=0, tiled=True),
        lax.all_gather(value_weight, ("fsdp", "ctx"), axis=0, tiled=True),
        lax.all_gather(output_weight, ("fsdp", "ctx"), axis=0, tiled=True),
        lax.all_gather(gate_weight, ("fsdp", "ctx"), axis=0, tiled=True),
        lax.all_gather(up_projection_weight, ("fsdp", "ctx"), axis=0, tiled=True),
        lax.all_gather(down_weight, ("fsdp", "ctx"), axis=0, tiled=True),
    )
    query_back, key_back, value_back, output_back, gate_back, up_back, down_back = back_weights
    upstream = cotangent.astype(jnp.float32)
    ffn_gain_grad = jnp.sum(upstream * mixed_unit, axis=(0, 1))
    mixed_grad = norm_back(upstream * feedforward_gain, mixed_unit, mixed_scale).astype(
        jnp.bfloat16
    )
    mixed_grad_block = gather_tokens(mixed_grad)
    inner_grad = project(mixed_grad_block, down_back)
    down_wgrad = weight_term(mixed_grad_block, mixed)
    gate_lin_grad = (inner_grad * up_lin * gate_sig * (1.0 + gate_lin * (1.0 - gate_sig))).astype(
        jnp.bfloat16
    )
    up_lin_grad = (inner_grad * gate_act).astype(jnp.bfloat16)
    gate_wgrad = weight_term(hidden_block, gate_lin_grad)
    up_wgrad = weight_term(hidden_block, up_lin_grad)
    hidden_grad = upstream + sum_tokens(
        project_back(gate_lin_grad, gate_back) + project_back(up_lin_grad, up_back)
    )
    attn_gain_grad = jnp.sum(hidden_grad * attention_unit, axis=(0, 1))
    attention_grad = norm_back(
        hidden_grad * attention_gain, attention_unit, attention_scale
    ).astype(jnp.bfloat16)
    attention_grad_block = gather_tokens(attention_grad)
    attended_output_gradient = project(attention_grad_block, output_back).astype(jnp.bfloat16)
    output_wgrad = weight_term(attention_grad_block, attended_block)
    attended_grad_heads = lax.all_to_all(
        heads_of(attended_output_gradient), "ctx", split_axis=2, concat_axis=1, tiled=True
    )
    probs_full = jnp.exp(masked_scores() - log_total)
    probs_again = probs_full.astype(jnp.bfloat16)
    value_grad_heads = jnp.einsum(
        "shqk,sqhd->skhd", probs_again, attended_grad_heads, preferred_element_type=jnp.float32
    ).astype(jnp.bfloat16)
    prob_grad = jnp.einsum(
        "sqhd,skhd->shqk", attended_grad_heads, value_heads, preferred_element_type=jnp.float32
    )
    delta_rows = jnp.einsum(
        "sqhd,sqhd->shq", attended_grad_heads, attended, preferred_element_type=jnp.float32
    )
    score_grad = (probs_full * (prob_grad - delta_rows[..., None])).astype(jnp.bfloat16)
    query_grad_heads = (
        jnp.einsum("shqk,skhd->sqhd", score_grad, key_heads, preferred_element_type=jnp.float32)
        * score_scale
    ).astype(jnp.bfloat16)
    key_grad_heads = (
        jnp.einsum("shqk,sqhd->skhd", score_grad, query_heads, preferred_element_type=jnp.float32)
        * score_scale
    ).astype(jnp.bfloat16)
    query_grad_rot, key_grad_rot, value_grad_rot = (
        lax.all_to_all(query_grad_heads, "ctx", split_axis=1, concat_axis=2, tiled=True),
        lax.all_to_all(key_grad_heads, "ctx", split_axis=1, concat_axis=2, tiled=True),
        lax.all_to_all(value_grad_heads, "ctx", split_axis=1, concat_axis=2, tiled=True),
    )
    query_grad_n = unrotate(query_grad_rot.astype(jnp.float32), cosine, sine).reshape(
        seq_count, block_len, width_local
    )
    key_grad_n = unrotate(key_grad_rot.astype(jnp.float32), cosine, sine).reshape(
        seq_count, block_len, width_local
    )
    query_gain_part = jnp.sum(query_grad_n * query_unit, axis=(0, 1))
    key_gain_part = jnp.sum(key_grad_n * key_unit, axis=(0, 1))
    query_grad_u = query_grad_n * query_gain_local
    key_grad_u = key_grad_n * key_gain_local
    query_inner, key_inner = lax.psum(
        (jnp.sum(query_grad_u * query_unit, axis=-1), jnp.sum(key_grad_u * key_unit, axis=-1)),
        "tensor",
    )
    query_pre = (query_scale * (query_grad_u - query_unit * (query_inner / D)[..., None])).astype(
        jnp.bfloat16
    )
    key_pre = (key_scale * (key_grad_u - key_unit * (key_inner / D)[..., None])).astype(
        jnp.bfloat16
    )
    value_pre = value_grad_rot.reshape(seq_count, block_len, width_local)
    input_attn = sum_tokens(
        project_back(query_pre, query_back)
        + project_back(key_pre, key_back)
        + project_back(value_pre, value_back)
    )
    input_grad = hidden_grad + input_attn
    query_wgrad = weight_term(tokens_block, query_pre)
    key_wgrad = weight_term(tokens_block, key_pre)
    value_wgrad = weight_term(tokens_block, value_pre)
    query_gain_full = lax.dynamic_update_slice_in_dim(
        jnp.zeros((D,), jnp.float32), query_gain_part, gain_start, 0
    )
    key_gain_full = lax.dynamic_update_slice_in_dim(
        jnp.zeros((D,), jnp.float32), key_gain_part, gain_start, 0
    )
    query_gain_grad, key_gain_grad, attention_gain_grad, feedforward_gain_grad = lax.psum(
        (query_gain_full, key_gain_full, attn_gain_grad, ffn_gain_grad), ("fsdp", "ctx", "tensor")
    )
    (
        query_reduced,
        key_reduced,
        value_reduced,
        output_reduced,
        gate_reduced,
        up_reduced,
        down_reduced,
    ) = (
        lax.psum_scatter(query_wgrad, ("fsdp", "ctx"), scatter_dimension=0, tiled=True),
        lax.psum_scatter(key_wgrad, ("fsdp", "ctx"), scatter_dimension=0, tiled=True),
        lax.psum_scatter(value_wgrad, ("fsdp", "ctx"), scatter_dimension=0, tiled=True),
        lax.psum_scatter(output_wgrad, ("fsdp", "ctx"), scatter_dimension=0, tiled=True),
        lax.psum_scatter(gate_wgrad, ("fsdp", "ctx"), scatter_dimension=0, tiled=True),
        lax.psum_scatter(up_wgrad, ("fsdp", "ctx"), scatter_dimension=0, tiled=True),
        lax.psum_scatter(down_wgrad, ("fsdp", "ctx"), scatter_dimension=0, tiled=True),
    )
    return (
        block_out,
        input_grad,
        query_reduced,
        key_reduced,
        value_reduced,
        output_reduced,
        gate_reduced,
        up_reduced,
        down_reduced,
        query_gain_grad,
        key_gain_grad,
        attention_gain_grad,
        feedforward_gain_grad,
    )


def solution(mesh):
    in_specs = (
        P("fsdp", ("ctx", "tensor"), None),
        P("fsdp", None),
        P("fsdp", None),
        P(("fsdp", "ctx"), "tensor"),
        P(("fsdp", "ctx"), "tensor"),
        P(("fsdp", "ctx"), "tensor"),
        P(("fsdp", "ctx"), "tensor"),
        P(("fsdp", "ctx"), "tensor"),
        P(("fsdp", "ctx"), "tensor"),
        P(("fsdp", "ctx"), "tensor"),
        P(),
        P(),
        P(),
        P(),
        P("fsdp", ("ctx", "tensor"), None),
    )
    out_specs = (
        P("fsdp", ("ctx", "tensor"), None),
        P("fsdp", ("ctx", "tensor"), None),
        P(("fsdp", "ctx"), "tensor"),
        P(("fsdp", "ctx"), "tensor"),
        P(("fsdp", "ctx"), "tensor"),
        P(("fsdp", "ctx"), "tensor"),
        P(("fsdp", "ctx"), "tensor"),
        P(("fsdp", "ctx"), "tensor"),
        P(("fsdp", "ctx"), "tensor"),
        P(),
        P(),
        P(),
        P(),
    )
    return jax.shard_map(body, mesh=mesh, in_specs=in_specs, out_specs=out_specs, check_vma=False)
```

profile of v0, /device:TPU:0, one launch (start us, length us, event | category | flops | bytes accessed | tf_op | source)
XLA Modules:
  0.0 1508.3 jit_solution(17496973479163622820)
XLA Ops:
  14.5 43.4 %all-gather.12.cloned.1.call-done = bf16[2,256,2048]{2,1,0:T(8,128)(2,1)} async-done(((bf16[2,64,2048]{2,1,0:T(8,128)(2,1)}), bf16[2,256,2048]{2,1,0:T(8,128)(2,1)}) %all-gather.12.cloned.1.call-update) | async-done | bytes 2097168 | tf_op jit(solution)/shard_map/all_gather | solution.py:73
  58.0 28.5 %all-gather.16.cloned.1.call-done = bf16[2048,512]{1,0:T(8,128)(2,1)} async-done(((bf16[256,512]{1,0:T(8,128)(2,1)}), bf16[2048,512]{1,0:T(8,128)(2,1)}) %all-gather.16.cloned.1.call-update) | async-done | bytes 2097168 | tf_op jit(solution)/shard_map/all_gather | solution.py:100
  90.0 26.1 %all-gather.18.cloned.1.call-done = bf16[2048,512]{1,0:T(8,128)(2,1)} async-done(((bf16[256,512]{1,0:T(8,128)(2,1)}), bf16[2048,512]{1,0:T(8,128)(2,1)}) %all-gather.18.cloned.1.call-update) | async-done | bytes 2097168 | tf_op jit(solution)/shard_map/all_gather | solution.py:101
  116.2 3.8 multiply_reduce_fusion.7
  120.0 11.7 all-reduce.2
  135.3 3.9 fusion.62
  151.6 4.4 all-to-all-done.2
  166.1 4.1 all-to-all-start
  174.0 7.8 all-to-all-done
  185.3 4.0 fusion.63
  195.3 10.6 all_to_all.108
  209.1 4.8 fusion.19
  214.8 75.6 %reduce-scatter.12.cloned.1.call-done = f32[2,64,2048]{2,1,0:T(8,128)} async-done(((f32[2,256,2048]{2,1,0:T(8,128)}), f32[2,64,2048]{2,1,0:T(8,128)}) %reduce-scatter.12.cloned.1.call-update) | async-done | bytes 1048592 | tf_op jit(solution)/shard_map/reduce_scatter | solution.py:77
  295.9 51.1 %all-gather.24.cloned.1.call-done = bf16[2048,2048]{1,0:T(8,128)(2,1)} async-done(((bf16[256,2048]{1,0:T(8,128)(2,1)}), bf16[2048,2048]{1,0:T(8,128)(2,1)}) %all-gather.24.cloned.1.call-update) | async-done | bytes 8388624 | tf_op jit(solution)/shard_map/all_gather | solution.py:104
  347.0 47.8 %all-gather.22.cloned.1.call-done = bf16[2,256,2048]{2,1,0:T(8,128)(2,1)} async-done(((bf16[2,64,2048]{2,1,0:T(8,128)(2,1)}), bf16[2,256,2048]{2,1,0:T(8,128)(2,1)}) %all-gather.22.cloned.1.call-update) | async-done | bytes 2097168 | tf_op jit(solution)/shard_map/all_gather | solution.py:73
  394.8 10.6 fusion.10
  405.4 44.4 %all-gather.26.cloned.1.call-done = bf16[2048,2048]{1,0:T(8,128)(2,1)} async-done(((bf16[256,2048]{1,0:T(8,128)(2,1)}), bf16[2048,2048]{1,0:T(8,128)(2,1)}) %all-gather.26.cloned.1.call-update) | async-done | bytes 8388624 | tf_op jit(solution)/shard_map/all_gather | solution.py:105
  449.8 12.5 multiply_convert_fusion.3
  462.3 43.5 %all-gather.28.cloned.1.call-done = bf16[2048,2048]{1,0:T(8,128)(2,1)} async-done(((bf16[256,2048]{1,0:T(8,128)(2,1)}), bf16[2048,2048]{1,0:T(8,128)(2,1)}) %all-gather.28.cloned.1.call-update) | async-done | bytes 8388624 | tf_op jit(solution)/shard_map/all_gather | solution.py:106
  505.8 10.5 fusion.2
  516.5 76.9 %reduce-scatter.14.cloned.1.call-done = f32[2,64,2048]{2,1,0:T(8,128)} async-done(((f32[2,256,2048]{2,1,0:T(8,128)}), f32[2,64,2048]{2,1,0:T(8,128)}) %reduce-scatter.14.cloned.1.call-update) | async-done | bytes 1048592 | tf_op jit(solution)/shard_map/reduce_scatter | solution.py:77
  598.9 46.1 %all-gather.30.cloned.1.call-done = bf16[2,256,2048]{2,1,0:T(8,128)(2,1)} async-done(((bf16[2,64,2048]{2,1,0:T(8,128)(2,1)}), bf16[2,256,2048]{2,1,0:T(8,128)(2,1)}) %all-gather.30.cloned.1.call-update) | async-done | bytes 2097168 | tf_op jit(solution)/shard_map/all_gather | solution.py:73
  645.0 11.9 multiply_convert_fusion.2
  656.9 8.5 fusion.4
  665.4 9.5 fusion.14
  675.0 75.7 %reduce-scatter.16.cloned.1.call-done = f32[2,64,2048]{2,1,0:T(8,128)} async-done(((f32[2,256,2048]{2,1,0:T(8,128)}), f32[2,64,2048]{2,1,0:T(8,128)}) %reduce-scatter.16.cloned.1.call-update) | async-done | bytes 1048592 | tf_op jit(solution)/shard_map/reduce_scatter | solution.py:77
  756.2 46.3 %all-gather.32.cloned.1.call-done = bf16[2,256,2048]{2,1,0:T(8,128)(2,1)} async-done(((bf16[2,64,2048]{2,1,0:T(8,128)(2,1)}), bf16[2,256,2048]{2,1,0:T(8,128)(2,1)}) %all-gather.32.cloned.1.call-update) | async-done | bytes 2097168 | tf_op jit(solution)/shard_map/all_gather | solution.py:73
  806.0 11.8 all_to_all.109
  817.9 5.7 fusion.50
  824.9 9.8 all_to_all.110
  843.9 6.0 multiply_convert_fusion
  853.8 4.1 all-to-all-start.5
  857.9 3.7 fusion.42
  862.7 4.1 all-to-all-done.5
  866.9 4.2 all-to-all-start.6
  872.2 9.2 all-to-all-done.6
  886.2 10.2 all-reduce.1
  919.0 4.9 convolution_bitcast_fusion.3
  923.9 12.6 convolution_bitcast_fusion
  938.1 9.8 convolution_bitcast_fusion.2
  948.2 9.8 convolution_bitcast_fusion.1
  958.5 39.2 %all-reduce = (f32[2048]{0:T(1024)}, f32[2048]{0:T(1024)}, f32[2048]{0:T(1024)}, f32[2048]{0:T(1024)}) all-reduce(f32[2048]{0:T(1024)S(1)} %dynamic_update_slice.6, f32[2048]{0:T(1024)S(1)} %dynamic_update_slice.7, f32[2048]{0:T(1024)S(1)} %get-tuple-element.52, ...), channel_id=1, replica_groups=mesh['fsdp'=2,'ctx'=4,'tensor'=4] {'fsdp','ctx','tensor'}, use_global_device_ids=true, to_apply=%region_26.27 | all-reduce | flops 8192 | bytes 65536 | tf_op jit(solution)/shard_map/psum | solution.py:280
  1001.8 3.9 reduce-scatter.20.cloned.1.call-done
  1007.8 76.9 %reduce-scatter.18.cloned.1.call-done = f32[2,64,2048]{2,1,0:T(8,128)} async-done(((f32[2,256,2048]{2,1,0:T(8,128)}), f32[2,64,2048]{2,1,0:T(8,128)}) %reduce-scatter.18.cloned.1.call-update) | async-done | bytes 1048592 | tf_op jit(solution)/shard_map/reduce_scatter | solution.py:77
  1087.1 53.2 %reduce-scatter.26.cloned.1.call-done = f32[256,512]{1,0:T(8,128)} async-done(((f32[2048,512]{1,0:T(8,128)}), f32[256,512]{1,0:T(8,128)}) %reduce-scatter.26.cloned.1.call-update) | async-done | bytes 524304 | tf_op jit(solution)/shard_map/reduce_scatter | solution.py:295
  1140.3 120.2 %reduce-scatter.32.cloned.1.call-done = f32[256,2048]{1,0:T(8,128)} async-done(((f32[2048,2048]{1,0:T(8,128)}), f32[256,2048]{1,0:T(8,128)}) %reduce-scatter.32.cloned.1.call-update) | async-done | bytes 2097168 | tf_op jit(solution)/shard_map/reduce_scatter | solution.py:298
  1260.5 120.4 %reduce-scatter.28.cloned.1.call-done = f32[256,2048]{1,0:T(8,128)} async-done(((f32[2048,2048]{1,0:T(8,128)}), f32[256,2048]{1,0:T(8,128)}) %reduce-scatter.28.cloned.1.call-update) | async-done | bytes 2097168 | tf_op jit(solution)/shard_map/reduce_scatter | solution.py:296
  1380.9 120.4 %reduce-scatter.30.cloned.1.call-done = f32[256,2048]{1,0:T(8,128)} async-done(((f32[2048,2048]{1,0:T(8,128)}), f32[256,2048]{1,0:T(8,128)}) %reduce-scatter.30.cloned.1.call-update) | async-done | bytes 2097168 | tf_op jit(solution)/shard_map/reduce_scatter | solution.py:297
  (210 shorter events, 129.2 us)
Async XLA Ops:
  7.2 50.8 %all-gather.12.cloned.1.call-start = ((), (), s32[]{:S(2)}) async-start(), calls=%async_computation.19 | async-start | bytes 2621440 | tf_op jit(solution)/shard_map/all_gather | solution.py:73
  7.9 78.6 %all-gather.16.cloned.1.call-start = ((), (), s32[]{:S(2)}) async-start(), calls=%async_computation.21 | async-start | bytes 2359296 | tf_op jit(solution)/shard_map/all_gather | solution.py:100
  8.7 107.5 %all-gather.18.cloned.1.call-start = ((), (), s32[]{:S(2)}) async-start(), calls=%async_computation.22 | async-start | bytes 2359296 | tf_op jit(solution)/shard_map/all_gather | solution.py:101
  9.4 150.1 %all-gather.14.cloned.1.call-start = ((), (), s32[]{:S(2)}) async-start(), calls=%async_computation.20 | async-start | bytes 2359296 | tf_op jit(solution)/shard_map/all_gather | solution.py:102
  10.0 198.3 %all-gather.20.cloned.1.call-start = ((), (), s32[]{:S(2)}) async-start(), calls=%async_computation.23 | async-start | bytes 2359296 | tf_op jit(solution)/shard_map/all_gather | solution.py:103
  58.0 58.2 %copy-start.2 = (bf16[2,256,2048]{2,1,0:T(8,128)(2,1)S(1)}, bf16[2,256,2048]{2,1,0:T(8,128)(2,1)}, u32[]{:S(2)}) copy-start(bf16[2,256,2048]{2,1,0:T(8,128)(2,1)} %all-gather.12.cloned.1.call-done) | copy-start | bytes 6291460
  90.0 42.8 %copy-start.9 = (f32[2,256,512]{2,1,0:T(8,128)}, f32[2,256,512]{2,1,0:T(8,128)S(1)}, u32[]{:S(2)}) copy-start(f32[2,256,512]{2,1,0:T(8,128)S(1)} %get-tuple-element.91) | copy-start | bytes 3145732
  135.3 3.9 copy-start.11
  146.0 10.0 all-to-all-start.2
  156.0 10.1 all-to-all-start.1
  162.3 22.9 %copy-start.38 = (s32[2,1024]{1,0:T(2,128)S(1)}, s32[2,1024]{1,0:T(2,128)}, u32[]{:S(2)}) copy-start(s32[2,1024]{1,0:T(2,128)} %param.16) | copy-start | bytes 24580
  166.1 5.8 copy-start.31
  166.1 15.7 %all-to-all-start = ((bf16[2,256,4,128]{3,1,0,2:T(8,128)(2,1)}), bf16[2,256,4,128]{3,1,0,2:T(8,128)(2,1)}, u32[]{:S(2)}, u32[]{:S(2)}) async-start(bf16[2,256,4,128]{3,1,0,2:T(8,128)(2,1)} %bitcast.218), calls=%async_computation | async-start | bytes 1048576 | tf_op jit(solution)/shard_map/all_to_all | solution.py:141
  170.2 120.1 %reduce-scatter.12.cloned.1.call-start = ((), (), s32[]{:S(2)}) async-start(), calls=%async_computation.24 | async-start | bytes 5242880 | tf_op jit(solution)/shard_map/reduce_scatter | solution.py:77
  171.9 17.4 %copy-start.16 = (bf16[2,4,256,1,128]{4,2,1,0,3:T(8,128)(2,1)}, bf16[2,4,256,1,128]{4,2,1,0,3:T(8,128)(2,1)S(1)}, u32[]{:S(2)}) copy-start(bf16[2,4,256,1,128]{4,2,1,0,3:T(8,128)(2,1)S(1)} %copy.93) | copy-start | bytes 1572868
  185.3 5.2 copy-start.19
  194.1 19.8 %copy-start.14 = (bf16[2,128,1024]{2,1,0:T(8,128)(2,1)}, bf16[2,128,1024]{2,1,0:T(8,128)(2,1)S(1)}, u32[]{:S(2)}) copy-start(bf16[2,128,1024]{2,1,0:T(8,128)(2,1)S(1)} %convolution_convert_fusion.1) | copy-start | bytes 1572868
  213.9 77.8 %copy-start.18 = (bf16[2,64,2048]{2,1,0:T(8,128)(2,1)S(1)}, bf16[2,64,2048]{2,1,0:T(8,128)(2,1)}, u32[]{:S(2)}) copy-start(bf16[2,64,2048]{2,1,0:T(8,128)(2,1)} %param.15) | copy-start | bytes 1572868
  213.9 77.8 %copy-start.35 = (f32[2048]{0:T(1024)S(1)}, f32[2048]{0:T(1024)}, u32[]{:S(2)}) copy-start(f32[2048]{0:T(1024)} %param.27) | copy-start | bytes 24580
  214.0 133.1 %all-gather.24.cloned.1.call-start = ((), (), s32[]{:S(2)}) async-start(), calls=%async_computation.26 | async-start | bytes 9437184 | tf_op jit(solution)/shard_map/all_gather | solution.py:104
  214.7 180.1 %all-gather.22.cloned.1.call-start = ((), (), s32[]{:S(2)}) async-start(), calls=%async_computation.25 | async-start | bytes 2621440 | tf_op jit(solution)/shard_map/all_gather | solution.py:73
  294.0 155.8 %all-gather.26.cloned.1.call-start = ((), (), s32[]{:S(2)}) async-start(), calls=%async_computation.27 | async-start | bytes 9437184 | tf_op jit(solution)/shard_map/all_gather | solution.py:105
  294.7 211.1 %all-gather.28.cloned.1.call-start = ((), (), s32[]{:S(2)}) async-start(), calls=%async_computation.28 | async-start | bytes 9437184 | tf_op jit(solution)/shard_map/all_gather | solution.py:106
  295.3 298.0 %reduce-scatter.14.cloned.1.call-start = ((), (), s32[]{:S(2)}) async-start(), calls=%async_computation.29 | async-start | bytes 5242880 | tf_op jit(solution)/shard_map/reduce_scatter | solution.py:77
  516.4 78.4 %copy-start.4 = (bf16[2,64,2048]{2,1,0:T(8,128)(2,1)S(1)}, bf16[2,64,2048]{2,1,0:T(8,128)(2,1)}, u32[]{:S(2)}) copy-start(bf16[2,64,2048]{2,1,0:T(8,128)(2,1)} %param.29) | copy-start | bytes 1572868
  516.4 78.4 %copy-start.36 = (f32[2048]{0:T(1024)S(1)}, f32[2048]{0:T(1024)}, u32[]{:S(2)}) copy-start(f32[2048]{0:T(1024)} %param.28) | copy-start | bytes 24580
  516.4 128.6 %all-gather.30.cloned.1.call-start = ((), (), s32[]{:S(2)}) async-start(), calls=%async_computation.30 | async-start | bytes 2621440 | tf_op jit(solution)/shard_map/all_gather | solution.py:73
  598.7 152.0 %reduce-scatter.16.cloned.1.call-start = ((), (), s32[]{:S(2)}) async-start(), calls=%async_computation.31 | async-start | bytes 5242880 | tf_op jit(solution)/shard_map/reduce_scatter | solution.py:77
  656.9 8.5 copy-start.39
  656.9 8.5 copy-start.40
  674.9 77.8 %copy-start.3 = (f32[2,64,2048]{2,1,0:T(8,128)S(1)}, f32[2,64,2048]{2,1,0:T(8,128)}, u32[]{:S(2)}) copy-start(f32[2,64,2048]{2,1,0:T(8,128)} %reduce-scatter.14.cloned.1.call-done) | copy-start | bytes 3145732
  675.0 127.5 %all-gather.32.cloned.1.call-start = ((), (), s32[]{:S(2)}) async-start(), calls=%async_computation.32 | async-start | bytes 2621440 | tf_op jit(solution)/shard_map/all_gather | solution.py:73
  756.1 241.7 %reduce-scatter.24.cloned.1.call-start = ((), (), s32[]{:S(2)}) async-start(), calls=%async_computation.36 | async-start | bytes 4718592 | tf_op jit(solution)/shard_map/reduce_scatter | solution.py:294
  843.8 8.0 copy-start.17
  851.9 6.0 copy-start.29
  853.8 13.1 all-to-all-start.5
  866.9 14.5 all-to-all-start.6
  871.0 128.8 %reduce-scatter.22.cloned.1.call-start = ((), (), s32[]{:S(2)}) async-start(), calls=%async_computation.35 | async-start | bytes 4718592 | tf_op jit(solution)/shard_map/reduce_scatter | solution.py:293
  902.8 102.9 %reduce-scatter.20.cloned.1.call-start = ((), (), s32[]{:S(2)}) async-start(), calls=%async_computation.34 | async-start | bytes 4718592 | tf_op jit(solution)/shard_map/reduce_scatter | solution.py:292
  905.7 3.8 copy-start.21
  909.0 3.7 copy-start.23
  909.0 175.7 %reduce-scatter.18.cloned.1.call-start = ((), (), s32[]{:S(2)}) async-start(), calls=%async_computation.33 | async-start | bytes 5242880 | tf_op jit(solution)/shard_map/reduce_scatter | solution.py:77
  918.0 222.3 %reduce-scatter.26.cloned.1.call-start = ((), (), s32[]{:S(2)}) async-start(), calls=%async_computation.37 | async-start | bytes 4718592 | tf_op jit(solution)/shard_map/reduce_scatter | solution.py:295
  923.9 336.7 %reduce-scatter.32.cloned.1.call-start = ((), (), s32[]{:S(2)}) async-start(), calls=%async_computation.40 | async-start | bytes 18874368 | tf_op jit(solution)/shard_map/reduce_scatter | solution.py:298
  936.5 444.4 %reduce-scatter.28.cloned.1.call-start = ((), (), s32[]{:S(2)}) async-start(), calls=%async_computation.38 | async-start | bytes 18874368 | tf_op jit(solution)/shard_map/reduce_scatter | solution.py:296
  948.0 553.3 %reduce-scatter.30.cloned.1.call-start = ((), (), s32[]{:S(2)}) async-start(), calls=%async_computation.39 | async-start | bytes 18874368 | tf_op jit(solution)/shard_map/reduce_scatter | solution.py:297
  958.0 126.7 %copy-start.5 = (bf16[2,64,2048]{2,1,0:T(8,128)(2,1)S(1)}, bf16[2,64,2048]{2,1,0:T(8,128)(2,1)}, u32[]{:S(2)}) copy-start(bf16[2,64,2048]{2,1,0:T(8,128)(2,1)} %param.29) | copy-start | bytes 1572868
  958.0 126.7 %copy-start.13 = (f32[2,64,2048]{2,1,0:T(8,128)S(1)}, f32[2,64,2048]{2,1,0:T(8,128)}, u32[]{:S(2)}) copy-start(f32[2,64,2048]{2,1,0:T(8,128)} %reduce-scatter.16.cloned.1.call-done) | copy-start | bytes 3145732
  (20 other events, 32.0 us)
Sparse Core Ops, SparseCore 0:
  9.6 48.3 all-gather.11
  59.9 26.5 all-gather.15
  88.4 27.7 all-gather.17
  117.9 27.7 all-gather.13
  147.4 35.7 all-gather.19
  214.1 76.1 reduce-scatter.11
  292.2 54.7 all-gather.23
  349.1 45.6 all-gather.21
  396.7 53.0 all-gather.25
  451.6 54.2 all-gather.27
  516.5 76.7 reduce-scatter.13
  598.8 46.1 all-gather.29
  675.1 75.5 reduce-scatter.15
  756.2 46.1 all-gather.31
  841.4 54.3 reduce-scatter.23
  902.9 48.2 reduce-scatter.21
  954.5 51.2 reduce-scatter.19
  1007.9 76.7 reduce-scatter.17
  1088.6 51.6 reduce-scatter.25
  1144.3 116.1 reduce-scatter.31
  1264.7 116.1 reduce-scatter.27
  1385.1 116.1 reduce-scatter.29
where the time goes:
time: 1520 us; the launch traced here: 1510 us
  waiting for transfers between devices  1130 us (74%)
  matrix products  159 us (10%)
  blocking collectives  93.2 us (6%)
  local copies, waits for them, and re-layouts  49.8 us (3%)
  other arithmetic  35.7 us (2%)
  starting transfers between devices  21.8 us (1%)
    reduce_scatter x4, waiting for transfers between devices, sum_tokens(): return lax.psum_scatter(terms, 'tensor', scatter_dimension=1, tiled=True)  305 us
    all_gather x4, waiting for transfers between devices, gather_tokens(): return lax.all_gather(matrix_rows, 'tensor', axis=1, tiled=True)  184 us
    reduce_scatter x1, waiting for transfers between devices, body(): lax.psum_scatter(gate_wgrad, ('fsdp', 'ctx'), scatter_dimension=0, tiled=...  120 us
    reduce_scatter x1, waiting for transfers between devices, body(): lax.psum_scatter(up_wgrad, ('fsdp', 'ctx'), scatter_dimension=0, tiled=True)  120 us
    reduce_scatter x1, waiting for transfers between devices, body(): lax.psum_scatter(down_wgrad, ('fsdp', 'ctx'), scatter_dimension=0, tiled=...  120 us
    reduce_scatter x1, waiting for transfers between devices, body(): lax.psum_scatter(output_wgrad, ('fsdp', 'ctx'), scatter_dimension=0, tile...  53.2 us
    all_gather x1, waiting for transfers between devices, body(): lax.all_gather(gate_weight, ('fsdp', 'ctx'), axis=0, tiled=True)  51.1 us
    dot_general x7, matrix products, project(): jnp.einsum('xmj,je->xme', matrix_rows, weight_matrix, preferred_element_t...  48.6 us
  transfers between devices with their start and end apart: 27, of which 23 were waited for; matrix products, arithmetic and copies ran while one was open for 11% of the time, Pallas kernels for 0%

commit v1 on v0

--- a/solution.py
+++ b/solution.py
@@ -8,6 +8,18 @@
 epsilon = 1e-06
 rope_theta = 500000.0
 masked_score = -1e30
+
+
+def doubled_up(value, axis, dim):
+    ways, here, step = (lax.axis_size(axis), lax.axis_index(axis), value.shape[dim])
+    line, have = (value, 1)
+    while have < ways:
+        line = jnp.concatenate(
+            [line, lax.ppermute(line, axis, [(d, (d - have) % ways) for d in range(ways)])],
+            axis=dim,
+        )
+        have = 2 * have
+    return jnp.roll(line, here * step, axis=dim)
 
 
 def rope_tables(position_ids):
@@ -70,7 +82,7 @@
 
 
 def gather_tokens(matrix_rows):
-    return lax.all_gather(matrix_rows, "tensor", axis=1, tiled=True)
+    return doubled_up(matrix_rows, "tensor", 1)
 
 
 def sum_tokens(terms):

time: 1520 us -> 1510 us (level)
  starting transfers between devices: 21.8 us -> 46.7 us
  local copies, waits for them, and re-layouts: 49.8 us -> 32.5 us
  other arithmetic: 35.7 us -> 51 us
    ppermute x0 -> x8, waiting for transfers between devices: none -> 222 us  [doubled_up(): lax.ppermute(line, axis, [(d, (d - have) % ways) for d in range(ways)])]
    all_gather x4 -> x0, waiting for transfers between devices: 184 us -> none  [gather_tokens(): return lax.all_gather(matrix_rows, 'tensor', axis=1, tiled=True)]
    reduce_scatter x4, waiting for transfers between devices: 305 us -> 226 us  [sum_tokens(): return lax.psum_scatter(terms, 'tensor', scatter_dimension=1, tiled=True)]
    reduce_scatter x1, waiting for transfers between devices: 0.01 us -> 55.1 us  [body(): lax.psum_scatter(value_wgrad, ('fsdp', 'ctx'), scatter_dimension=0, tiled...]
    reduce_scatter x1, waiting for transfers between devices: 0.01 us -> 55 us  [body(): lax.psum_scatter(key_wgrad, ('fsdp', 'ctx'), scatter_dimension=0, tiled=T...]
    reduce_scatter x1, waiting for transfers between devices: 3.87 us -> 55 us  [body(): lax.psum_scatter(query_wgrad, ('fsdp', 'ctx'), scatter_dimension=0, tiled...]
    all_gather x1, waiting for transfers between devices: 51.1 us -> 0.02 us  [body(): lax.all_gather(gate_weight, ('fsdp', 'ctx'), axis=0, tiled=True)]
    all_gather x1, waiting for transfers between devices: 28.5 us -> 0.02 us  [body(): lax.all_gather(query_weight, ('fsdp', 'ctx'), axis=0, tiled=True)]
  transfers between devices with their start and end apart: 27 -> 32, of which waited for: 23 -> 25; matrix products, arithmetic and copies ran while one was open for 11% -> 9% of each run, Pallas kernels for 0% -> 0%
where the time goes in v1:
time: 1510 us; the launch traced here: 1500 us
  waiting for transfers between devices  1120 us (74%)
  matrix products  146 us (10%)
  blocking collectives  85.9 us (6%)
  other arithmetic  51 us (3%)
  starting transfers between devices  46.7 us (3%)
  local copies, waits for them, and re-layouts  32.5 us (2%)
  between operations  15.5 us (1%)
    reduce_scatter x4, waiting for transfers between devices, sum_tokens(): return lax.psum_scatter(terms, 'tensor', scatter_dimension=1, tiled=True)  226 us
    ppermute x8, waiting for transfers between devices, doubled_up(): lax.ppermute(line, axis, [(d, (d - have) % ways) for d in range(ways)])  222 us
    reduce_scatter x1, waiting for transfers between devices, body(): lax.psum_scatter(up_wgrad, ('fsdp', 'ctx'), scatter_dimension=0, tiled=True)  120 us
    reduce_scatter x1, waiting for transfers between devices, body(): lax.psum_scatter(down_wgrad, ('fsdp', 'ctx'), scatter_dimension=0, tiled=...  120 us
    reduce_scatter x1, waiting for transfers between devices, body(): lax.psum_scatter(gate_wgrad, ('fsdp', 'ctx'), scatter_dimension=0, tiled=...  120 us
    reduce_scatter x1, waiting for transfers between devices, body(): lax.psum_scatter(value_wgrad, ('fsdp', 'ctx'), scatter_dimension=0, tiled...  55.1 us
    reduce_scatter x1, waiting for transfers between devices, body(): lax.psum_scatter(key_wgrad, ('fsdp', 'ctx'), scatter_dimension=0, tiled=T...  55 us
    reduce_scatter x1, waiting for transfers between devices, body(): lax.psum_scatter(query_wgrad, ('fsdp', 'ctx'), scatter_dimension=0, tiled...  55 us
  transfers between devices with their start and end apart: 32, of which 25 were waited for; matrix products, arithmetic and copies ran while one was open for 9% of the time, Pallas kernels for 0%

profile of v1, /device:TPU:0, one launch (start us, length us, event | category | flops | bytes accessed | tf_op | source)
XLA Modules:
  0.0 1499.1 jit_solution(5970796328032420266)
XLA Ops:
  9.4 5.1 collective-permute-start
  14.6 11.5 collective-permute-done
  32.6 42.2 %collective-permute-done.1 = bf16[2,128,2048]{2,1,0:T(8,128)(2,1)} collective-permute-done((bf16[2,128,2048]{2,1,0:T(8,128)(2,1)S(1)}, bf16[2,128,2048]{2,1,0:T(8,128)(2,1)}, u32[]{:S(2)}, u32[]{:S(2)}) %collective-permute-start.1) | collective-permute-done | bytes 1048608 | tf_op jit(solution)/shard_map/ppermute | solution.py:18
  74.8 4.9 fusion.34
  87.4 10.8 all-reduce.2
  113.1 6.8 all-to-all-done.2
  127.2 8.6 all-to-all-done.1
  141.1 6.0 all-to-all-done
  156.9 10.0 all_to_all.108
  167.6 5.1 fusion.39
  174.9 71.5 %reduce-scatter.12.cloned.1.call-done = f32[2,64,2048]{2,1,0:T(8,128)} async-done(((f32[2,256,2048]{2,1,0:T(8,128)}), f32[2,64,2048]{2,1,0:T(8,128)}) %reduce-scatter.12.cloned.1.call-update) | async-done | bytes 1048592 | tf_op jit(solution)/shard_map/reduce_scatter | solution.py:89
  252.1 11.3 collective-permute-done.2
  266.1 44.9 %collective-permute-done.3 = bf16[2,128,2048]{2,1,0:T(8,128)(2,1)S(1)} collective-permute-done((bf16[2,128,2048]{2,1,0:T(8,128)(2,1)S(1)}, bf16[2,128,2048]{2,1,0:T(8,128)(2,1)S(1)}, u32[]{:S(2)}, u32[]{:S(2)}) %collective-permute-start.3) | collective-permute-done | bytes 1048608 | tf_op jit(solution)/shard_map/ppermute | solution.py:18
  311.1 4.9 fusion.29
  316.1 10.1 fusion.10
  326.2 33.0 %all-gather.18.cloned.1.call-done = bf16[2048,2048]{1,0:T(8,128)(2,1)} async-done(((bf16[256,2048]{1,0:T(8,128)(2,1)}), bf16[2048,2048]{1,0:T(8,128)(2,1)}) %all-gather.18.cloned.1.call-update) | async-done | bytes 8388624 | tf_op jit(solution)/shard_map/all_gather | solution.py:117
  359.1 10.8 multiply_convert_fusion.3
  369.9 45.4 %all-gather.20.cloned.1.call-done = bf16[2048,2048]{1,0:T(8,128)(2,1)} async-done(((bf16[256,2048]{1,0:T(8,128)(2,1)}), bf16[2048,2048]{1,0:T(8,128)(2,1)}) %all-gather.20.cloned.1.call-update) | async-done | bytes 8388624 | tf_op jit(solution)/shard_map/all_gather | solution.py:118
  415.3 10.6 fusion.2
  425.9 76.9 %reduce-scatter.14.cloned.1.call-done = f32[2,64,2048]{2,1,0:T(8,128)} async-done(((f32[2,256,2048]{2,1,0:T(8,128)}), f32[2,64,2048]{2,1,0:T(8,128)}) %reduce-scatter.14.cloned.1.call-update) | async-done | bytes 1048592 | tf_op jit(solution)/shard_map/reduce_scatter | solution.py:89
  510.4 11.3 collective-permute-done.4
  524.4 45.0 %collective-permute-done.5 = bf16[2,128,2048]{2,1,0:T(8,128)(2,1)S(1)} collective-permute-done((bf16[2,128,2048]{2,1,0:T(8,128)(2,1)S(1)}, bf16[2,128,2048]{2,1,0:T(8,128)(2,1)S(1)}, u32[]{:S(2)}, u32[]{:S(2)}) %collective-permute-start.5) | collective-permute-done | bytes 1048608 | tf_op jit(solution)/shard_map/ppermute | solution.py:18
  569.4 5.0 fusion.24
  574.4 11.4 multiply_convert_fusion.2
  585.9 6.2 fusion.4
  592.1 8.4 fusion.14
  600.5 77.8 %reduce-scatter.16.cloned.1.call-done = f32[2,64,2048]{2,1,0:T(8,128)} async-done(((f32[2,256,2048]{2,1,0:T(8,128)}), f32[2,64,2048]{2,1,0:T(8,128)}) %reduce-scatter.16.cloned.1.call-update) | async-done | bytes 1048592 | tf_op jit(solution)/shard_map/reduce_scatter | solution.py:89
  685.5 11.3 collective-permute-done.6
  699.6 44.9 %collective-permute-done.7 = bf16[2,128,2048]{2,1,0:T(8,128)(2,1)S(1)} collective-permute-done((bf16[2,128,2048]{2,1,0:T(8,128)(2,1)S(1)}, bf16[2,128,2048]{2,1,0:T(8,128)(2,1)S(1)}, u32[]{:S(2)}, u32[]{:S(2)}) %collective-permute-start.7) | collective-permute-done | bytes 1048608 | tf_op jit(solution)/shard_map/ppermute | solution.py:18
  744.6 4.9 fusion.19
  750.9 10.5 all_to_all.109
  764.0 5.2 multiply_convert_fusion
  786.7 4.9 fusion.70
  798.6 6.2 all-to-all-done.7
  812.2 13.8 all-reduce.1
  836.9 4.9 convolution_bitcast_fusion.3
  846.2 4.4 convolution_bitcast_fusion.5
  855.6 9.8 convolution_bitcast_fusion
  867.0 9.8 convolution_bitcast_fusion.2
  876.9 9.9 convolution_bitcast_fusion.1
  887.3 40.7 %all-reduce = (f32[2048]{0:T(1024)}, f32[2048]{0:T(1024)}, f32[2048]{0:T(1024)}, f32[2048]{0:T(1024)}) all-reduce(f32[2048]{0:T(1024)S(1)} %dynamic_update_slice.6, f32[2048]{0:T(1024)S(1)} %dynamic_update_slice.7, f32[2048]{0:T(1024)S(1)} %get-tuple-element.14, ...), channel_id=1, replica_groups=mesh['fsdp'=2,'ctx'=4,'tensor'=4] {'fsdp','ctx','tensor'}, use_global_device_ids=true, to_apply=%region_26.28 | all-reduce | flops 8192 | bytes 65536 | tf_op jit(solution)/shard_map/psum | solution.py:292
  930.5 35.8 %reduce-scatter.26.cloned.1.call-done = f32[256,512]{1,0:T(8,128)} async-done(((f32[2048,512]{1,0:T(8,128)}), f32[256,512]{1,0:T(8,128)}) %reduce-scatter.26.cloned.1.call-update) | async-done | bytes 524304 | tf_op jit(solution)/shard_map/reduce_scatter | solution.py:307
  966.2 55.1 %reduce-scatter.24.cloned.1.call-done = f32[256,512]{1,0:T(8,128)} async-done(((f32[2048,512]{1,0:T(8,128)}), f32[256,512]{1,0:T(8,128)}) %reduce-scatter.24.cloned.1.call-update) | async-done | bytes 524304 | tf_op jit(solution)/shard_map/reduce_scatter | solution.py:306
  1021.4 55.0 %reduce-scatter.22.cloned.1.call-done = f32[256,512]{1,0:T(8,128)} async-done(((f32[2048,512]{1,0:T(8,128)}), f32[256,512]{1,0:T(8,128)}) %reduce-scatter.22.cloned.1.call-update) | async-done | bytes 524304 | tf_op jit(solution)/shard_map/reduce_scatter | solution.py:305
  1076.3 55.0 %reduce-scatter.20.cloned.1.call-done = f32[256,512]{1,0:T(8,128)} async-done(((f32[2048,512]{1,0:T(8,128)}), f32[256,512]{1,0:T(8,128)}) %reduce-scatter.20.cloned.1.call-update) | async-done | bytes 524304 | tf_op jit(solution)/shard_map/reduce_scatter | solution.py:304
  1131.3 120.2 %reduce-scatter.32.cloned.1.call-done = f32[256,2048]{1,0:T(8,128)} async-done(((f32[2048,2048]{1,0:T(8,128)}), f32[256,2048]{1,0:T(8,128)}) %reduce-scatter.32.cloned.1.call-update) | async-done | bytes 2097168 | tf_op jit(solution)/shard_map/reduce_scatter | solution.py:310
  1251.5 120.2 %reduce-scatter.28.cloned.1.call-done = f32[256,2048]{1,0:T(8,128)} async-done(((f32[2048,2048]{1,0:T(8,128)}), f32[256,2048]{1,0:T(8,128)}) %reduce-scatter.28.cloned.1.call-update) | async-done | bytes 2097168 | tf_op jit(solution)/shard_map/reduce_scatter | solution.py:308
  1371.8 120.2 %reduce-scatter.30.cloned.1.call-done = f32[256,2048]{1,0:T(8,128)} async-done(((f32[2048,2048]{1,0:T(8,128)}), f32[256,2048]{1,0:T(8,128)}) %reduce-scatter.30.cloned.1.call-update) | async-done | bytes 2097168 | tf_op jit(solution)/shard_map/reduce_scatter | solution.py:309
  (258 shorter events, 145.3 us)
Async XLA Ops:
  7.2 72.6 %all-gather.10.cloned.1.call-start = ((), (), s32[]{:S(2)}) async-start(), calls=%async_computation.20 | async-start | bytes 2359296 | tf_op jit(solution)/shard_map/all_gather | solution.py:112
  7.9 75.5 %all-gather.12.cloned.1.call-start = ((), (), s32[]{:S(2)}) async-start(), calls=%async_computation.21 | async-start | bytes 2359296 | tf_op jit(solution)/shard_map/all_gather | solution.py:113
  8.7 114.8 %all-gather.8.cloned.1.call-start = ((), (), s32[]{:S(2)}) async-start(), calls=%async_computation.19 | async-start | bytes 2359296 | tf_op jit(solution)/shard_map/all_gather | solution.py:114
  9.4 158.2 %all-gather.14.cloned.1.call-start = ((), (), s32[]{:S(2)}) async-start(), calls=%async_computation.22 | async-start | bytes 2359296 | tf_op jit(solution)/shard_map/all_gather | solution.py:115
  9.4 16.6 %collective-permute-start = (bf16[2,64,2048]{2,1,0:T(8,128)(2,1)}, bf16[2,64,2048]{2,1,0:T(8,128)(2,1)S(1)}, u32[]{:S(2)}, u32[]{:S(2)}) collective-permute-start(bf16[2,64,2048]{2,1,0:T(8,128)(2,1)} %param.17), channel_id=1, source_target_pairs={{0,3},{1,0},{2,1},{3,2},{4,7},{5,4},{6,5},{7,6},{8,11},{9,8},{10,9... | collective-permute-start | bytes 1572872 | tf_op jit(solution)/shard_map/ppermute | solution.py:18
  27.2 47.6 %collective-permute-start.1 = (bf16[2,128,2048]{2,1,0:T(8,128)(2,1)S(1)}, bf16[2,128,2048]{2,1,0:T(8,128)(2,1)}, u32[]{:S(2)}, u32[]{:S(2)}) collective-permute-start(bf16[2,128,2048]{2,1,0:T(8,128)(2,1)S(1)} %pad_maximum_fusion), channel_id=1, source_target_pairs={{0,2},{1,3},{2,0},{3,1},{4,6},{5,7},{6,4},{7,5},{8,10},{9,11},{10,... | collective-permute-start | bytes 3145736 | tf_op jit(solution)/shard_map/ppermute | solution.py:18
  106.1 17.4 %copy-start.33 = (bf16[2,256,2048]{2,1,0:T(8,128)(2,1)S(1)}, bf16[2,256,2048]{2,1,0:T(8,128)(2,1)}, u32[]{:S(2)}) copy-start(bf16[2,256,2048]{2,1,0:T(8,128)(2,1)} %copy-done.32) | copy-start | bytes 6291460
  107.2 12.7 all-to-all-start.2
  119.9 15.9 %all-to-all-start.1 = ((bf16[2,256,4,128]{3,1,0,2:T(8,128)(2,1)}), bf16[2,256,4,128]{3,1,0,2:T(8,128)(2,1)S(1)}, u32[]{:S(2)}, u32[]{:S(2)}) async-start(bf16[2,256,4,128]{3,1,0,2:T(8,128)(2,1)} %copy.90), calls=%async_computation.1 | async-start | bytes 1048576 | tf_op jit(solution)/shard_map/all_to_all | solution.py:151
  126.3 21.5 %copy-start.52 = (s32[2,1024]{1,0:T(2,128)S(1)}, s32[2,1024]{1,0:T(2,128)}, u32[]{:S(2)}) copy-start(s32[2,1024]{1,0:T(2,128)} %param.18) | copy-start | bytes 24580
  135.7 11.4 all-to-all-start
  139.2 107.2 %reduce-scatter.12.cloned.1.call-start = ((), (), s32[]{:S(2)}) async-start(), calls=%async_computation.23 | async-start | bytes 5242880 | tf_op jit(solution)/shard_map/reduce_scatter | solution.py:89
  172.7 75.0 %copy-start.17 = (bf16[2,64,2048]{2,1,0:T(8,128)(2,1)S(1)}, bf16[2,64,2048]{2,1,0:T(8,128)(2,1)}, u32[]{:S(2)}) copy-start(bf16[2,64,2048]{2,1,0:T(8,128)(2,1)} %param.17) | copy-start | bytes 1572868
  172.7 75.0 %copy-start.50 = (f32[2048]{0:T(1024)S(1)}, f32[2048]{0:T(1024)}, u32[]{:S(2)}) copy-start(f32[2048]{0:T(1024)} %param.29) | copy-start | bytes 24580
  172.8 143.3 %all-gather.16.cloned.1.call-start = ((), (), s32[]{:S(2)}) async-start(), calls=%async_computation.24 | async-start | bytes 9437184 | tf_op jit(solution)/shard_map/all_gather | solution.py:116
  173.3 185.8 %all-gather.18.cloned.1.call-start = ((), (), s32[]{:S(2)}) async-start(), calls=%async_computation.25 | async-start | bytes 9437184 | tf_op jit(solution)/shard_map/all_gather | solution.py:117
  174.1 241.2 %all-gather.20.cloned.1.call-start = ((), (), s32[]{:S(2)}) async-start(), calls=%async_computation.26 | async-start | bytes 9437184 | tf_op jit(solution)/shard_map/all_gather | solution.py:118
  174.8 328.0 %reduce-scatter.14.cloned.1.call-start = ((), (), s32[]{:S(2)}) async-start(), calls=%async_computation.27 | async-start | bytes 5242880 | tf_op jit(solution)/shard_map/reduce_scatter | solution.py:89
  249.2 14.2 collective-permute-start.2
  263.5 47.6 %collective-permute-start.3 = (bf16[2,128,2048]{2,1,0:T(8,128)(2,1)S(1)}, bf16[2,128,2048]{2,1,0:T(8,128)(2,1)S(1)}, u32[]{:S(2)}, u32[]{:S(2)}) collective-permute-start(bf16[2,128,2048]{2,1,0:T(8,128)(2,1)S(1)} %pad_maximum_fusion.1), channel_id=1, source_target_pairs={{0,2},{1,3},{2,0},{3,1},{4,6},{5,7},{6,4},{7,5},{8,10},{9,11},{10,... | collective-permute-start | bytes 3145736 | tf_op jit(solution)/shard_map/ppermute | solution.py:18
  316.0 43.1 %copy-start.36 = (bf16[2,256,2048]{2,1,0:T(8,128)(2,1)}, bf16[2,256,2048]{2,1,0:T(8,128)(2,1)S(1)}, u32[]{:S(2)}) copy-start(bf16[2,256,2048]{2,1,0:T(8,128)(2,1)S(1)} %fusion.29) | copy-start | bytes 6291460
  425.9 78.3 %copy-start.4 = (bf16[2,64,2048]{2,1,0:T(8,128)(2,1)S(1)}, bf16[2,64,2048]{2,1,0:T(8,128)(2,1)}, u32[]{:S(2)}) copy-start(bf16[2,64,2048]{2,1,0:T(8,128)(2,1)} %param.31) | copy-start | bytes 1572868
  425.9 78.3 %copy-start.51 = (f32[2048]{0:T(1024)S(1)}, f32[2048]{0:T(1024)}, u32[]{:S(2)}) copy-start(f32[2048]{0:T(1024)} %param.30) | copy-start | bytes 24580
  425.9 252.5 %reduce-scatter.16.cloned.1.call-start = ((), (), s32[]{:S(2)}) async-start(), calls=%async_computation.28 | async-start | bytes 5242880 | tf_op jit(solution)/shard_map/reduce_scatter | solution.py:89
  505.9 68.5 %copy-start.54 = (f32[2,256,2048]{2,1,0:T(8,128)S(1)}, f32[2,256,2048]{2,1,0:T(8,128)}, u32[]{:S(2)}) copy-start(f32[2,256,2048]{2,1,0:T(8,128)} %fusion.10) | copy-start | bytes 12582916
  507.5 14.2 collective-permute-start.4
  521.8 47.6 %collective-permute-start.5 = (bf16[2,128,2048]{2,1,0:T(8,128)(2,1)S(1)}, bf16[2,128,2048]{2,1,0:T(8,128)(2,1)S(1)}, u32[]{:S(2)}, u32[]{:S(2)}) collective-permute-start(bf16[2,128,2048]{2,1,0:T(8,128)(2,1)S(1)} %pad_maximum_fusion.2), channel_id=1, source_target_pairs={{0,2},{1,3},{2,0},{3,1},{4,6},{5,7},{6,4},{7,5},{8,10},{9,11},{10,... | collective-permute-start | bytes 3145736 | tf_op jit(solution)/shard_map/ppermute | solution.py:18
  569.4 16.4 %slice-start.2 = ((s8[8388608]{0:T(1024)(128)(4,1)}), s8[4194304]{0:T(1024)(128)(4,1)S(1)}, s32[]{:S(2)}) async-start(s8[8388608]{0:T(1024)(128)(4,1)} %bitcast.220), calls=%async_computation.39 | async-start | bytes 8388608
  569.4 22.7 %slice-start = ((s8[8388608]{0:T(1024)(128)(4,1)}), s8[4194304]{0:T(1024)(128)(4,1)S(1)}, s32[]{:S(2)}) async-start(s8[8388608]{0:T(1024)(128)(4,1)} %bitcast.218), calls=%async_computation.37 | async-start | bytes 8388608
  574.4 17.7 %slice-start.1 = ((s8[8388608]{0:T(1024)(128)(4,1)}), s8[4194304]{0:T(1024)(128)(4,1)S(1)}, s32[]{:S(2)}) async-start(s8[8388608]{0:T(1024)(128)(4,1)} %bitcast.218), calls=%async_computation.38 | async-start | bytes 8388608
  600.5 77.9 %copy-start.3 = (f32[2,64,2048]{2,1,0:T(8,128)S(1)}, f32[2,64,2048]{2,1,0:T(8,128)}, u32[]{:S(2)}) copy-start(f32[2,64,2048]{2,1,0:T(8,128)} %reduce-scatter.12.cloned.1.call-done) | copy-start | bytes 3145732
  600.5 79.5 %copy-start.2 = (f32[2,64,2048]{2,1,0:T(8,128)S(1)}, f32[2,64,2048]{2,1,0:T(8,128)}, u32[]{:S(2)}) copy-start(f32[2,64,2048]{2,1,0:T(8,128)} %reduce-scatter.14.cloned.1.call-done) | copy-start | bytes 3145732
  682.6 66.9 %copy-start.35 = (bf16[2048,512]{1,0:T(8,128)(2,1)S(1)}, bf16[2048,512]{1,0:T(8,128)(2,1)}, u32[]{:S(2)}) copy-start(bf16[2048,512]{1,0:T(8,128)(2,1)} %all-gather.14.cloned.1.call-done) | copy-start | bytes 6291460
  682.6 14.3 collective-permute-start.6
  697.0 47.6 %collective-permute-start.7 = (bf16[2,128,2048]{2,1,0:T(8,128)(2,1)S(1)}, bf16[2,128,2048]{2,1,0:T(8,128)(2,1)S(1)}, u32[]{:S(2)}, u32[]{:S(2)}) collective-permute-start(bf16[2,128,2048]{2,1,0:T(8,128)(2,1)S(1)} %pad_maximum_fusion.3), channel_id=1, source_target_pairs={{0,2},{1,3},{2,0},{3,1},{4,6},{5,7},{6,4},{7,5},{8,10},{9,11},{10,... | collective-permute-start | bytes 3145736 | tf_op jit(solution)/shard_map/ppermute | solution.py:18
  773.2 10.0 all-to-all-start.5
  783.3 10.7 all-to-all-start.6
  794.0 10.9 all-to-all-start.7
  798.1 129.9 %reduce-scatter.18.cloned.1.call-start = ((), (), s32[]{:S(2)}) async-start(), calls=%async_computation.29 | async-start | bytes 5242880 | tf_op jit(solution)/shard_map/reduce_scatter | solution.py:89
  811.7 16.8 %copy-start.6 = (f32[2,256,4,64]{3,1,2,0:T(8,128)S(1)}, f32[2,256,4,64]{3,1,2,0:T(8,128)}, u32[]{:S(2)}) copy-start(f32[2,256,4,64]{3,1,2,0:T(8,128)} %copy-done.5) | copy-start | bytes 1572868
  835.9 130.3 %reduce-scatter.26.cloned.1.call-start = ((), (), s32[]{:S(2)}) async-start(), calls=%async_computation.33 | async-start | bytes 4718592 | tf_op jit(solution)/shard_map/reduce_scatter | solution.py:307
  841.8 179.5 %reduce-scatter.24.cloned.1.call-start = ((), (), s32[]{:S(2)}) async-start(), calls=%async_computation.32 | async-start | bytes 4718592 | tf_op jit(solution)/shard_map/reduce_scatter | solution.py:306
  846.2 230.2 %reduce-scatter.22.cloned.1.call-start = ((), (), s32[]{:S(2)}) async-start(), calls=%async_computation.31 | async-start | bytes 4718592 | tf_op jit(solution)/shard_map/reduce_scatter | solution.py:305
  850.6 280.7 %reduce-scatter.20.cloned.1.call-start = ((), (), s32[]{:S(2)}) async-start(), calls=%async_computation.30 | async-start | bytes 4718592 | tf_op jit(solution)/shard_map/reduce_scatter | solution.py:304
  854.0 397.5 %reduce-scatter.32.cloned.1.call-start = ((), (), s32[]{:S(2)}) async-start(), calls=%async_computation.36 | async-start | bytes 18874368 | tf_op jit(solution)/shard_map/reduce_scatter | solution.py:310
  865.4 506.3 %reduce-scatter.28.cloned.1.call-start = ((), (), s32[]{:S(2)}) async-start(), calls=%async_computation.34 | async-start | bytes 18874368 | tf_op jit(solution)/shard_map/reduce_scatter | solution.py:308
  876.8 615.2 %reduce-scatter.30.cloned.1.call-start = ((), (), s32[]{:S(2)}) async-start(), calls=%async_computation.35 | async-start | bytes 18874368 | tf_op jit(solution)/shard_map/reduce_scatter | solution.py:309
  886.8 41.3 %copy-start.16 = (f32[2,64,2048]{2,1,0:T(8,128)S(1)}, f32[2,64,2048]{2,1,0:T(8,128)}, u32[]{:S(2)}) copy-start(f32[2,64,2048]{2,1,0:T(8,128)} %reduce-scatter.16.cloned.1.call-done) | copy-start | bytes 3145732
  (43 other events, 240.4 us)
Sparse Core Ops, SparseCore 0:
  9.9 30.4 all-gather.9
  42.3 27.7 all-gather.11
  72.0 27.7 all-gather.7
  101.5 35.7 all-gather.13
  172.9 73.4 reduce-scatter.11
  248.1 54.7 all-gather.15
  304.8 54.2 all-gather.17
  361.0 54.2 all-gather.19
  426.0 76.7 reduce-scatter.13
  600.7 77.6 reduce-scatter.15
  836.1 74.4 reduce-scatter.17
  914.4 51.8 reduce-scatter.25
  970.2 51.1 reduce-scatter.23
  1025.1 51.1 reduce-scatter.21
  1080.1 51.1 reduce-scatter.19
  1135.3 116.1 reduce-scatter.31
  1255.5 116.1 reduce-scatter.27
  1375.8 116.2 reduce-scatter.29
